TPU v7x, 32 devices: a whole 2x2x4 slice. The times are simulated.
32 devices in a mesh: gx: 2 (over x), gy: 4 (over y, core), gz: 4 (over z).
Axes of the slice: x: 2, y: 2, z: 4, core: 2. Of those that a mesh axis runs over, the one named last changes fastest.
Arguments:
- features: bfloat16 [256, 4096], P('gz', ('gy', 'gx')), may hold values from -14 to 14, as said below
- tiles: bfloat16 [32, 32, 128, 128], P('gx', 'gy'), may hold values from -0.5 to 0.5
- block_mask: int32 [32, 32], P('gx', 'gy'), may hold values from 0 to 1, as said below
- tile_counts: int32 [32], P('gx'), may hold values from 1 to 32, as said below
- weight: bfloat16 [256, 256], replicated, may hold values from -0.375 to 0.375
- gamma: float32 [256], P('gz'), may hold values from 0.5 to 2
- beta: float32 [256], P('gz'), may hold values from -3 to 3
Outputs:
- normed: bfloat16 [256, 4096], P('gz', ('gx', 'gy'))
Inputs may be any that keep to these rules, and one draw needn't show every extreme that they name: `features`: channels along dimension 0, nodes along dimension 1. `block_mask`: 1 where block row and block column meet in a nonzero block, else 0; the diagonal is 1. tile_counts[r] is the number of ones in row r of block_mask.
All inputs are finite; a program needn't handle non-finite values.
Results may differ from a plain program's by a relative error of at most 0.013.
Values may be sent and summed in bfloat16 or wider, within the bound.
A program may use at most 64 MiB of HBM per device.

v0:
```python
import jax
import jax.numpy as jnp
from jax import lax
from jax.sharding import PartitionSpec as P


def body(features, tiles, block_mask, tile_counts, weight, gamma, beta):
    panel = lax.all_gather(features, "gx", axis=1, tiled=True)
    local_ch = panel.shape[0]
    rows_blk = tiles.shape[0]
    cols_blk = tiles.shape[1]
    tile_len = tiles.shape[2]
    panels = panel.reshape(local_ch, cols_blk, tile_len)
    prods = jnp.einsum("fcn,rcmn->frcm", panels, tiles, preferred_element_type=jnp.float32)
    share = block_mask.astype(jnp.float32) / tile_counts.astype(jnp.float32)[:, None]
    partial_value = jnp.einsum("frcm,rc->frm", prods, share).reshape(local_ch, rows_blk * tile_len)
    summed = lax.psum(partial_value, "gy")
    width = rows_blk * tile_len // lax.axis_size("gy")
    agg = lax.dynamic_slice_in_dim(summed, lax.axis_index("gy") * width, width, 1)
    agg = agg.astype(jnp.bfloat16)
    offset = lax.axis_index("gz") * local_ch
    full = lax.all_gather(agg, "gz", axis=0, tiled=True)
    w_cols = lax.dynamic_slice_in_dim(weight, offset, local_ch, 1)
    z_vals = jnp.einsum("co,cn->on", w_cols, full, preferred_element_type=jnp.float32)
    total = z_vals.shape[1] * lax.axis_size(("gx", "gy"))
    sums, squares = lax.psum(
        (jnp.sum(z_vals, axis=1), jnp.sum(z_vals * z_vals, axis=1)), ("gx", "gy")
    )
    mean = sums / total
    var = squares / total - mean * mean
    centered = z_vals - mean[:, None]
    scaled = gamma[:, None] * centered * lax.rsqrt(var + 1e-05)[:, None] + beta[:, None]
    return jnp.maximum(scaled, 0.0).astype(jnp.bfloat16)


def solution(mesh):
    in_specs = (
        P("gz", ("gy", "gx")),
        P("gx", "gy", None, None),
        P("gx", "gy"),
        P("gx"),
        P(),
        P("gz"),
        P("gz"),
    )
    out_specs = P("gz", ("gx", "gy"))
    return jax.shard_map(body, mesh=mesh, in_specs=in_specs, out_specs=out_specs, check_vma=False)
```

profile of v0, /device:TPU:0, one launch (start us, length us, event | category | flops | bytes accessed | tf_op | source)
XLA Modules:
  0.0 57.3 jit_solution(9171550169248883873)
XLA Ops:
  0.0 0.0 copy-start
  0.0 0.7 %convert_element_type.13 = f32[16]{0:T(128)S(1)} convert(s32[16]{0:T(128)} %param.10) | non-fusion elementwise | flops 16 | bytes 128 | tf_op jit(solution)/shard_map/convert_element_type | solution.py:15
  0.7 0.7 %divide_bitcast_fusion = bf16[16,8,1,1]{0,1,2,3:T(8,128)(2,1)S(1)} fusion(s32[16,8]{0,1:T(8,128)} %param.9, f32[16]{0:T(128)S(1)} %convert_element_type.13), kind=kLoop, calls=%fused_computation.12 | loop fusion | flops 384 | bytes 832 | tf_op jit(solution)/shard_map/div | solution.py:15
  1.4 0.1 copy.12
  1.5 6.1 %all_gather.6 = bf16[64,1024]{1,0:T(8,128)(2,1)S(1)} all-gather(bf16[64,512]{1,0:T(8,128)(2,1)} %param.7), channel_id=1, replica_groups=mesh['gx'=2,'gy'=4,'gz'=4] {'gx'}, dimensions={1}, use_global_device_ids=true | all-gather | bytes 196608 | tf_op jit(solution)/shard_map/all_gather | solution.py:8
  7.6 3.8 %fusion.4 = bf16[64,16,8,128]{3,0,1,2:T(8,128)(2,1)S(1)} fusion(bf16[16,8,128,128]{3,2,1,0:T(8,128)(2,1)} %param.8, bf16[64,8,128,1]{2,1,0,3:T(8,128)(2,1)S(1)} %bitcast.19), kind=kOutput, calls=%fused_computation.4 | convolution fusion | flops 268435456 | bytes 6422528 | tf_op jit(solution)/shard_map/fcn,rcmn->frcm/dot_general | solution.py:14
  11.4 1.4 %fusion = f32[16,1,64,128]{3,1,2,0:T(1,128)S(1)} fusion(bf16[16,8,1,1]{1,2,3,0:T(2,128)(2,1)S(1)} %copy.12, bf16[64,16,8,128]{3,0,1,2:T(8,128)(2,1)S(1)} %fusion.4), kind=kOutput, calls=%fused_computation | convolution fusion | flops 2097152 | bytes 2621696 | tf_op jit(solution)/shard_map/frcm,rc->frm/dot_general | solution.py:16
  12.8 0.0 copy-start.1
  12.8 0.0 copy-start.2
  12.8 0.3 copy.14
  13.2 0.2 copy.28
  13.3 16.7 %all-reduce.2 = bf16[64,2048]{1,0:T(8,128)(2,1)S(1)} all-reduce(f32[64,2048]{1,0:T(8,128)S(1)} %bitcast.18), channel_id=1, replica_groups=mesh['gx'=2,'gy'=4,'gz'=4] {'gy'}, use_global_device_ids=true, to_apply=%region_0.0 | all-reduce | flops 131072 | bytes 786432 | tf_op jit(solution)/shard_map/psum | solution.py:17
  30.1 14.2 %all_gather.7 = bf16[256,512]{1,0:T(8,128)(2,1)S(1)} all-gather(bf16[64,512]{1,0:T(8,128)(2,1)S(1)} %dynamic-slice_convert_fusion), channel_id=1, replica_groups=mesh['gx'=2,'gy'=4,'gz'=4] {'gz'}, dimensions={0}, use_global_device_ids=true | all-gather | bytes 327680 | tf_op jit(solution)/shard_map/all_gather | solution.py:22
  44.3 0.0 copy-done
  44.3 0.4 fusion.11
  44.7 11.8 %all-reduce = (f32[64]{0:T(128)S(1)}, f32[64]{0:T(128)S(1)}) all-reduce(f32[64]{0:T(128)S(1)} %get-tuple-element.6, f32[64]{0:T(128)S(1)} %get-tuple-element.5), channel_id=1, replica_groups=mesh['gx'=2,'gy'=4,'gz'=4] {'gx','gy'}, use_global_device_ids=true, to_apply=%region_4.0 | all-reduce | flops 128 | bytes 1024 | tf_op jit(solution)/shard_map/psum | solution.py:26
  56.5 0.0 copy-done.1
  56.5 0.0 copy-done.2
  56.5 0.7 %maximum_convert_fusion = bf16[64,512]{1,0:T(8,128)(2,1)} fusion(f32[64,512]{1,0:T(8,128)S(1)} %get-tuple-element.11, f32[64]{0:T(128)S(1)} %copy-done.1, f32[64]{0:T(128)S(1)} %get-tuple-element.10, f32[64]{0:T(128)S(1)} %get-tuple-element.9, f32[64]{0:T(128)S(1)} %copy-done.2), kind=kLoop, calls=%fused_computation.7 | loop fusion | flops 196608 | bytes 197632 | tf_op jit(solution)/shard_map/convert_element_type | solution.py:33
  (3 shorter events, 0.0 us)
Async XLA Ops:
  0.0 44.3 %copy-start = (bf16[256,256]{1,0:T(8,128)(2,1)S(1)}, bf16[256,256]{1,0:T(8,128)(2,1)}, u32[]{:S(2)}) copy-start(bf16[256,256]{1,0:T(8,128)(2,1)} %param.11) | copy-start | bytes 393220
  12.8 43.7 %copy-start.1 = (f32[64]{0:T(128)S(1)}, f32[64]{0:T(128)}, u32[]{:S(2)}) copy-start(f32[64]{0:T(128)} %param.13) | copy-start | bytes 772
  12.8 43.7 %copy-start.2 = (f32[64]{0:T(128)S(1)}, f32[64]{0:T(128)}, u32[]{:S(2)}) copy-start(f32[64]{0:T(128)} %param.12) | copy-start | bytes 772
where the time goes:
time: 57.5 us; the launch traced here: 57.3 us
  blocking collectives  48.9 us (85%)
  matrix products  5.54 us (10%)
  other arithmetic  2.13 us (4%)
  local copies, waits for them, and re-layouts  0.61 us (1%)
    psum x1, blocking collectives, body(): summed = lax.psum(partial_value, 'gy')  16.7 us
    all_gather x1, blocking collectives, body(): full = lax.all_gather(agg, 'gz', axis=0, tiled=True)  14.2 us
    psum x1, blocking collectives, body(): lax.psum((jnp.sum(z_vals, axis=1), jnp.sum(z_vals * z_vals, axis=1)), ('g...  11.8 us
    all_gather x1, blocking collectives, body(): panel = lax.all_gather(features, 'gx', axis=1, tiled=True)  6.13 us
    dot_general x1, matrix products, body(): jnp.einsum('fcn,rcmn->frcm', panels, tiles, preferred_element_type=jnp.fl...  3.75 us
    dot_general x1, matrix products, body(): jnp.einsum('frcm,rc->frm', prods, share)  1.42 us

commit v1 on v0

--- a/solution.py
+++ b/solution.py
@@ -2,6 +2,19 @@
 import jax.numpy as jnp
 from jax import lax
 from jax.sharding import PartitionSpec as P
+from jax.lax import axis_index, axis_size, ppermute
+
+
+def cover_units(local_values, axis_k=0):
+    shelf = [local_values]
+    n = axis_size("gz")
+    for c in [*range(n - 1)]:
+        shelf.append(ppermute(shelf[-1], "gz", [(nth, (nth + 1) % n) for nth in range(n)]))
+    return jnp.roll(
+        jnp.concatenate(shelf[::-1], axis=axis_k),
+        shift=(axis_index("gz") + 1) * local_values.shape[axis_k],
+        axis=axis_k,
+    )
 
 
 def body(features, tiles, block_mask, tile_counts, weight, gamma, beta):
@@ -19,7 +32,7 @@
     agg = lax.dynamic_slice_in_dim(summed, lax.axis_index("gy") * width, width, 1)
     agg = agg.astype(jnp.bfloat16)
     offset = lax.axis_index("gz") * local_ch
-    full = lax.all_gather(agg, "gz", axis=0, tiled=True)
+    full = cover_units(agg)
     w_cols = lax.dynamic_slice_in_dim(weight, offset, local_ch, 1)
     z_vals = jnp.einsum("co,cn->on", w_cols, full, preferred_element_type=jnp.float32)
     total = z_vals.shape[1] * lax.axis_size(("gx", "gy"))

time: 57.5 us -> 61.6 us (1.071)
  waiting for transfers between devices: 0 us -> 16.5 us
  blocking collectives: 48.9 us -> 34.7 us
  starting transfers between devices: 0 us -> 1.74 us
    ppermute x0 -> x3, waiting for transfers between devices: none -> 16.5 us  [cover_units(): ppermute(shelf[-1], 'gz', [(nth, (nth + 1) % n) for nth in range(n)])]
    all_gather x1 -> x0, blocking collectives: 14.2 us -> none  [body(): full = lax.all_gather(agg, 'gz', axis=0, tiled=True)]
    ppermute x0 -> x3, starting transfers between devices: none -> 1.74 us  [cover_units(): ppermute(shelf[-1], 'gz', [(nth, (nth + 1) % n) for nth in range(n)])]
  transfers between devices with their start and end apart: 0 -> 3, of which waited for: 0 -> 3; matrix products, arithmetic and copies ran while one was open for 0% -> 0% of each run, Pallas kernels for 0% -> 0%
where the time goes in v1:
time: 61.6 us; the launch traced here: 61.4 us
  blocking collectives  34.7 us (56%)
  waiting for transfers between devices  16.5 us (27%)
  matrix products  5.54 us (9%)
  other arithmetic  2.13 us (3%)
  starting transfers between devices  1.74 us (3%)
  local copies, waits for them, and re-layouts  0.68 us (1%)
    psum x1, blocking collectives, body(): summed = lax.psum(partial_value, 'gy')  16.7 us
    ppermute x3, waiting for transfers between devices, cover_units(): ppermute(shelf[-1], 'gz', [(nth, (nth + 1) % n) for nth in range(n)])  16.5 us
    psum x1, blocking collectives, body(): lax.psum((jnp.sum(z_vals, axis=1), jnp.sum(z_vals * z_vals, axis=1)), ('g...  11.8 us
    all_gather x1, blocking collectives, body(): panel = lax.all_gather(features, 'gx', axis=1, tiled=True)  6.13 us
    dot_general x1, matrix products, body(): jnp.einsum('fcn,rcmn->frcm', panels, tiles, preferred_element_type=jnp.fl...  3.75 us
    ppermute x3, starting transfers between devices, cover_units(): ppermute(shelf[-1], 'gz', [(nth, (nth + 1) % n) for nth in range(n)])  1.74 us
    dot_general x1, matrix products, body(): jnp.einsum('frcm,rc->frm', prods, share)  1.42 us
  transfers between devices with their start and end apart: 3, of which 3 were waited for; matrix products, arithmetic and copies ran while one was open for 0% of the time, Pallas kernels for 0%

profile of v1, /device:TPU:0, one launch (start us, length us, event | category | flops | bytes accessed | tf_op | source)
XLA Modules:
  0.0 61.4 jit_solution(4794866651375266219)
XLA Ops:
  0.0 0.0 copy-start
  0.0 0.7 %convert_element_type.13 = f32[16]{0:T(128)S(1)} convert(s32[16]{0:T(128)} %param.10) | non-fusion elementwise | flops 16 | bytes 128 | tf_op jit(solution)/shard_map/convert_element_type | solution.py:28
  0.7 0.7 %divide_bitcast_fusion = bf16[16,8,1,1]{0,1,2,3:T(8,128)(2,1)S(1)} fusion(s32[16,8]{0,1:T(8,128)} %param.9, f32[16]{0:T(128)S(1)} %convert_element_type.13), kind=kLoop, calls=%fused_computation.21 | loop fusion | flops 384 | bytes 832 | tf_op jit(solution)/shard_map/div | solution.py:28
  1.4 0.1 copy.12
  1.5 6.1 %all_gather.3 = bf16[64,1024]{1,0:T(8,128)(2,1)S(1)} all-gather(bf16[64,512]{1,0:T(8,128)(2,1)} %param.7), channel_id=1, replica_groups=mesh['gx'=2,'gy'=4,'gz'=4] {'gx'}, dimensions={1}, use_global_device_ids=true | all-gather | bytes 196608 | tf_op jit(solution)/shard_map/all_gather | solution.py:21
  7.6 3.8 %fusion.4 = bf16[64,16,8,128]{3,0,1,2:T(8,128)(2,1)S(1)} fusion(bf16[16,8,128,128]{3,2,1,0:T(8,128)(2,1)} %param.8, bf16[64,8,128,1]{2,1,0,3:T(8,128)(2,1)S(1)} %bitcast.18), kind=kOutput, calls=%fused_computation.4 | convolution fusion | flops 268435456 | bytes 6422528 | tf_op jit(solution)/shard_map/fcn,rcmn->frcm/dot_general | solution.py:27
  11.4 1.4 %fusion = f32[16,1,64,128]{3,1,2,0:T(1,128)S(1)} fusion(bf16[16,8,1,1]{1,2,3,0:T(2,128)(2,1)S(1)} %copy.12, bf16[64,16,8,128]{3,0,1,2:T(8,128)(2,1)S(1)} %fusion.4), kind=kOutput, calls=%fused_computation | convolution fusion | flops 2097152 | bytes 2621696 | tf_op jit(solution)/shard_map/frcm,rc->frm/dot_general | solution.py:29
  12.8 0.0 copy-start.1
  12.8 0.0 copy-start.2
  12.8 0.3 copy.14
  13.2 0.2 copy.28
  13.3 16.7 %all-reduce.2 = bf16[64,2048]{1,0:T(8,128)(2,1)S(1)} all-reduce(f32[64,2048]{1,0:T(8,128)S(1)} %bitcast.17), channel_id=1, replica_groups=mesh['gx'=2,'gy'=4,'gz'=4] {'gy'}, use_global_device_ids=true, to_apply=%region_0.0 | all-reduce | flops 131072 | bytes 786432 | tf_op jit(solution)/shard_map/psum | solution.py:30
  30.1 1.7 %collective-permute-start = (bf16[64,512]{1,0:T(8,128)(2,1)S(1)}, bf16[64,512]{1,0:T(8,128)(2,1)S(1)}, u32[]{:S(2)}, u32[]{:S(2)}) collective-permute-start(bf16[64,512]{1,0:T(8,128)(2,1)S(1)} %dynamic-slice_convert_fusion), channel_id=1, source_target_pairs={{0,1},{1,2},{2,3},{3,0},{4,5},{5,6},{6,7},{7,4},{8,9},{9,10},{10,1... | collective-permute-start | bytes 196616 | tf_op jit(solution)/shard_map/ppermute | solution.py:12
  31.8 4.4 %collective-permute-done = bf16[64,512]{1,0:T(8,128)(2,1)S(1)} collective-permute-done((bf16[64,512]{1,0:T(8,128)(2,1)S(1)}, bf16[64,512]{1,0:T(8,128)(2,1)S(1)}, u32[]{:S(2)}, u32[]{:S(2)}) %collective-permute-start) | collective-permute-done | bytes 65568 | tf_op jit(solution)/shard_map/ppermute | solution.py:12
  36.2 0.0 collective-permute-start.1
  36.2 6.1 %collective-permute-done.1 = bf16[64,512]{1,0:T(8,128)(2,1)S(1)} collective-permute-done((bf16[64,512]{1,0:T(8,128)(2,1)S(1)}, bf16[64,512]{1,0:T(8,128)(2,1)S(1)}, u32[]{:S(2)}, u32[]{:S(2)}) %collective-permute-start.1) | collective-permute-done | bytes 65568 | tf_op jit(solution)/shard_map/ppermute | solution.py:12
  42.3 0.0 collective-permute-start.2
  42.3 6.1 %collective-permute-done.2 = bf16[64,512]{1,0:T(8,128)(2,1)S(1)} collective-permute-done((bf16[64,512]{1,0:T(8,128)(2,1)S(1)}, bf16[64,512]{1,0:T(8,128)(2,1)S(1)}, u32[]{:S(2)}, u32[]{:S(2)}) %collective-permute-start.2) | collective-permute-done | bytes 65568 | tf_op jit(solution)/shard_map/ppermute | solution.py:12
  48.5 0.0 copy-done
  48.5 0.4 fusion.12
  48.9 11.8 %all-reduce = (f32[64]{0:T(128)S(1)}, f32[64]{0:T(128)S(1)}) all-reduce(f32[64]{0:T(128)S(1)} %get-tuple-element.6, f32[64]{0:T(128)S(1)} %get-tuple-element.5), channel_id=1, replica_groups=mesh['gx'=2,'gy'=4,'gz'=4] {'gx','gy'}, use_global_device_ids=true, to_apply=%region_4.5 | all-reduce | flops 128 | bytes 1024 | tf_op jit(solution)/shard_map/psum | solution.py:39
  60.7 0.0 copy-done.1
  60.7 0.0 copy-done.2
  60.7 0.7 %maximum_convert_fusion = bf16[64,512]{1,0:T(8,128)(2,1)} fusion(f32[64,512]{1,0:T(8,128)S(1)} %get-tuple-element.11, f32[64]{0:T(128)S(1)} %copy-done.1, f32[64]{0:T(128)S(1)} %get-tuple-element.10, f32[64]{0:T(128)S(1)} %get-tuple-element.9, f32[64]{0:T(128)S(1)} %copy-done.2), kind=kLoop, calls=%fused_computation.9 | loop fusion | flops 196608 | bytes 197632 | tf_op jit(solution)/shard_map/convert_element_type | solution.py:46
  (11 shorter events, 0.1 us)
Async XLA Ops:
  0.0 48.5 %copy-start = (bf16[256,256]{1,0:T(8,128)(2,1)S(1)}, bf16[256,256]{1,0:T(8,128)(2,1)}, u32[]{:S(2)}) copy-start(bf16[256,256]{1,0:T(8,128)(2,1)} %param.11) | copy-start | bytes 393220
  12.8 47.9 %copy-start.1 = (f32[64]{0:T(128)S(1)}, f32[64]{0:T(128)}, u32[]{:S(2)}) copy-start(f32[64]{0:T(128)} %param.13) | copy-start | bytes 772
  12.8 47.8 %copy-start.2 = (f32[64]{0:T(128)S(1)}, f32[64]{0:T(128)}, u32[]{:S(2)}) copy-start(f32[64]{0:T(128)} %param.12) | copy-start | bytes 772
  30.1 6.1 %collective-permute-start = (bf16[64,512]{1,0:T(8,128)(2,1)S(1)}, bf16[64,512]{1,0:T(8,128)(2,1)S(1)}, u32[]{:S(2)}, u32[]{:S(2)}) collective-permute-start(bf16[64,512]{1,0:T(8,128)(2,1)S(1)} %dynamic-slice_convert_fusion), channel_id=1, source_target_pairs={{0,1},{1,2},{2,3},{3,0},{4,5},{5,6},{6,7},{7,4},{8,9},{9,10},{10,1... | collective-permute-start | bytes 196616 | tf_op jit(solution)/shard_map/ppermute | solution.py:12
  36.2 6.1 %collective-permute-start.1 = (bf16[64,512]{1,0:T(8,128)(2,1)S(1)}, bf16[64,512]{1,0:T(8,128)(2,1)S(1)}, u32[]{:S(2)}, u32[]{:S(2)}) collective-permute-start(bf16[64,512]{1,0:T(8,128)(2,1)S(1)} %collective-permute-done), channel_id=1, source_target_pairs={{0,1},{1,2},{2,3},{3,0},{4,5},{5,6},{6,7},{7,4},{8,9},{9,10},{10,1... | collective-permute-start | bytes 196616 | tf_op jit(solution)/shard_map/ppermute | solution.py:12
  42.3 6.1 %collective-permute-start.2 = (bf16[64,512]{1,0:T(8,128)(2,1)S(1)}, bf16[64,512]{1,0:T(8,128)(2,1)S(1)}, u32[]{:S(2)}, u32[]{:S(2)}) collective-permute-start(bf16[64,512]{1,0:T(8,128)(2,1)S(1)} %collective-permute-done.1), channel_id=1, source_target_pairs={{0,1},{1,2},{2,3},{3,0},{4,5},{5,6},{6,7},{7,4},{8,9},{9,10},{10,1... | collective-permute-start | bytes 196616 | tf_op jit(solution)/shard_map/ppermute | solution.py:12
